TPU v7x, 32 devices: a whole 2x2x4 slice. The times are simulated.
32 devices in a mesh: grp: 4 (over z), gx: 8 (over y, x, core).
Axes of the slice: x: 2, y: 2, z: 4, core: 2. Of those that a mesh axis runs over, the one named last changes fastest.
Arguments:
- component_density: float32 [53, 256, 1024], P(None, 'gx', 'grp'), may hold values from 0.05 to 2
- scaled_thermal_state: float32 [256, 1024], P('gx', 'grp'), may hold values from 0.5 to 1.5
- leading_direction_flow: float32 [256, 1024], P('gx', 'grp'), may hold values from -1 to 1
- trailing_direction_flow: float32 [256, 1024], P('gx', 'grp'), may hold values from -1 to 1
- spreading_coefficient: float32 [54], replicated, may hold values from 0.02 to 0.2
- colliding_pair: int32 [325, 2], replicated, may hold values from 0 to 52
- natural_exponent_scaler: float32 [325], replicated, may hold values from -3 to -1
- arrhenius_energy: float32 [325], replicated, may hold values from 0 to 2
- stoichiometric_output: float32 [325, 53], replicated, may hold values from 0.004 to 0.075
- formation_warming: float32 [53], replicated, may hold values from -1.8 to 1.8
- explicit_increments: int32 [2048], P(('grp', 'gx')), may hold values from 1 to 4
Outputs:
- species_out: float32 [53, 256, 1024], P(None, 'gx', 'grp')
- temperature_out: float32 [256, 1024], P('gx', 'grp')
All inputs are finite; a program needn't handle non-finite values.
Results may differ from a plain program's by a relative error of at most 0.0003.
Values sent between devices are 32-bit elements; how exact they have to be, the bound alone decides.
A program may use at most 64 MiB of HBM per device.

v0:
```python
import functools
import math

import jax
import jax.numpy as jnp
import numpy as np
from jax import lax
from jax.experimental import pallas as pl
from jax.experimental.pallas import tpu as pltpu
from jax.sharding import PartitionSpec as P

TILE = 128
FIRST_SCALE = 60.0
SECOND_SCALE = 180.0
transport_step = 0.4
chemistry_span = 0.5
sixth_first = (0.75, -0.15, 1.0 / 60.0)
sixth_second = (1.5, -0.15, 1.0 / 90.0)
sixth_center = -49.0 / 18.0


def up(n, m):
    return -(-n // m) * m


def spread_weights(reactions):
    golden = (math.sqrt(5.0) - 1.0) / 2.0
    return np.exp2((np.arange(reactions) * golden) % 1.0).astype(np.float32)


REACH = 3
SLOT = 4
LANES = 128
NEVER = -16384.0
TRIPS = 3
ROOM = 32 << 20


def halves(value):
    high = value.astype(jnp.bfloat16)
    return high, (value - high.astype(jnp.float32)).astype(jnp.bfloat16)


def prepare_tables(pair, scaler, energy, produced, weight, counts, rates, table, offsets, order, lines):
    reactions = pair.shape[1]
    length = rates.shape[0] // 3
    species = produced.shape[0]
    half = table.shape[0] // 2
    scale = 1.0 / math.log(2.0)
    wide = lines.shape[1]
    lines[...] = jnp.zeros_like(lines)
    lines[0:1, :] = jnp.full((1, wide), NEVER)
    lines[0, 0:reactions] = scaler[...] * scale
    lines[1, 0:reactions] = energy[...] * scale
    lines[2:3, 0:reactions] = weight[...]
    for n in range(3):
        for r in range(0, length, LANES):
            count = min(LANES, length - r)
            row = jnp.broadcast_to(lines[n:n + 1, r:r + LANES], (LANES, LANES))
            rates[n * length + r:n * length + r + count, :] = row.T[:count]
    table[...] = jnp.zeros_like(table)
    high, low = halves(produced[...] / weight[...])
    table[0:species, 0:reactions] = high
    table[half:half + species, 0:reactions] = low
    offsets[...] = jnp.zeros_like(offsets)
    for n in range(2):
        offsets[:, n * wide:n * wide + reactions] = pair[n:n + 1, :] * PITCH
    tiles = counts.shape[1]
    lines[3:4, 0:tiles] = counts[...].astype(jnp.float32) * tiles
    key = lines[3:4, 0:LANES] + lax.broadcasted_iota(jnp.int32, (1, LANES), 1).astype(jnp.float32)
    down = lax.broadcasted_iota(jnp.int32, (LANES, LANES), 0).astype(jnp.float32)
    along = lax.broadcasted_iota(jnp.int32, (LANES, LANES), 1)
    across = jnp.broadcast_to(key, (LANES, LANES))
    before = jnp.where((across < across.T) & (along < tiles), 1.0, 0.0)
    rank = jnp.sum(before, axis=1, keepdims=True)
    here = jnp.where((rank == along.astype(jnp.float32)) & (down < tiles), down, 0.0)
    order[...] = jnp.sum(here, axis=0, keepdims=True).astype(jnp.int32)


def advect_kernel(fields, sizes, density, warm, leading, trailing, diffusion, band, pair, scaler, energy, produced,
                  weight, counts, out, rates, table, offsets, order,
                  lines, spread, start, one, two, east, north, pieces, across, packed, landed, flows, send, recv):
    n_grp, n_gx = sizes
    g, x = lax.axis_index("grp"), lax.axis_index("gx")
    rows, cols = warm.shape
    parts = cols // LANES
    tiles = start.shape[0] // parts
    species = fields - 1
    last = fields // 8
    up, down = (g, lax.rem(x + n_gx - 1, n_gx)), (g, lax.rem(x + 1, n_gx))
    left, right = (lax.rem(g + n_grp - 1, n_grp), x), (lax.rem(g + 1, n_grp), x)
    barrier = pltpu.get_barrier_semaphore()
    for place in (up, down, left, right):
        pl.semaphore_signal(barrier, inc=1, device_id=place, device_id_type=pl.DeviceIdType.MESH)

    lane = lax.broadcasted_iota(jnp.int32, (8, LANES), 1)
    slot = lane % SLOT
    home = LANES - SLOT * rows

    def at(row):
        return pl.ds(row * 8 if isinstance(row, int) else pl.multiple_of(row * 8, 8), 8)

    def spread_out(read, t, sub):
        for q in range(rows // 8):
            for h in range(parts):
                start[t * parts + h, pl.ds((REACH + q * 8) * 8 + sub, 8, stride=8), :] = read(q, h)

    def of_density(f):
        return lambda q, h: density[pl.ds(pl.multiple_of(f * rows + q * 8, 8), 8), h * LANES:(h + 1) * LANES]

    def of_plane(ref):
        return lambda q, h: ref[q * 8:(q + 1) * 8, h * LANES:(h + 1) * LANES]

    def copies(s, t):
        held = (start, one, two)[s]
        both = pl.ds(t * parts, parts)
        plan = [
            (held.at[both, pl.ds(REACH * 8, REACH * 8)], held.at[both, pl.ds((REACH + rows) * 8, REACH * 8)], up),
            (held.at[both, pl.ds(rows * 8, REACH * 8)], held.at[both, pl.ds(0, REACH * 8)], down),
            (packed.at[s, t, 0], landed.at[s, t, 1], left),
            (packed.at[s, t, 1], landed.at[s, t, 0], right),
        ]
        return [pltpu.make_async_remote_copy(
            src_ref=src, dst_ref=dst, send_sem=send.at[s, t, n], recv_sem=recv.at[s, t, n],
            device_id=place, device_id_type=pl.DeviceIdType.MESH) for n, (src, dst, place) in enumerate(plan)]

    def pack(s, t):
        held = (start, one, two)[s]
        def merge(low, count, part, join):
            if count == 1:
                return held[t * parts + part, at(REACH + low), :]
            here = count // 2
            return join(merge(low, here, part, join), here, merge(low + here, count - here, part, join), count - here)

        def from_left(a, n, b, m):
            return jnp.where(lane < SLOT * n, a, pltpu.roll(b, SLOT * n, 1))

        def from_right(a, n, b, m):
            return jnp.where(lane >= LANES - SLOT * m, b, pltpu.roll(a, LANES - SLOT * m, 1))

        first = merge(0, rows, 0, from_left)
        final = merge(0, rows, parts - 1, from_right)
        packed[s, t, 0] = first
        packed[s, t, 1] = final
        for copy in copies(s, t):
            copy.start()

    for f in range(tiles * 8):
        spread[f:f + 1, :] = jnp.full((1, LANES), diffusion[f] if f < fields else 0.0)
    for f in range(last * 8, species):
        spread_out(of_density(f), last, f % 8)
    for n, ref in enumerate((warm, leading, trailing)):
        spread_out(of_plane(ref), last, (species + n) % 8)
    pl.semaphore_wait(barrier, 4)
    pack(0, last)

    def prepare(t, c):
        for sub in range(8):
            spread_out(of_density(t * 8 + sub), t, sub)
        pack(0, t)
        return c

    lax.fori_loop(0, last, prepare, 0)

    pull, push = transport_step * sixth_first[0], -transport_step / FIRST_SCALE
    for i in range(rows):
        for h in range(parts):
            lanes = slice(h * LANES, (h + 1) * LANES)
            east[h, at(REACH + i), :] = jnp.broadcast_to(pull * leading[i:i + 1, lanes], (8, LANES))
            north[h, at(i), :] = jnp.broadcast_to(push * trailing[i:i + 1, lanes], (8, LANES))

    def arrive(s, t):
        for copy in copies(s, t):
            copy.wait_recv()

    prepare_tables(pair, scaler, energy, produced, weight, counts, rates, table, offsets, order, lines)
    arrive(0, last)
    u_sub, v_sub = fields % 8, (fields + 1) % 8
    for r in (*range(REACH), *range(REACH + rows, 2 * REACH + rows)):
        for h in range(parts):
            east[h, at(r), :] = jnp.broadcast_to(
                pull * start[last * parts + h, pl.ds(r * 8 + u_sub, 1), :], (8, LANES))
    for side in range(2):
        flow = jnp.broadcast_to(landed[0, last, side, pl.ds(v_sub, 1), :], (8, LANES))
        for k in range(1, REACH + 1):
            inside = slot >= SLOT - k if side == 0 else slot < k
            weight = (1.0 if side == 0 else -1.0) * transport_step * sixth_first[k - 1]
            flows[side * REACH + k - 1] = jnp.where(inside, weight * flow, 0.0)

    def split(held, t):
        scale = spread[at(t), :] * (transport_step / SECOND_SCALE)
        for i in range(rows):
            fs = [held[t * parts + h, at(REACH + i), :] for h in range(parts)]
            f_high, f_low = halves(jnp.concatenate([scale * f for f in fs], 1))
            g_high, g_low = halves(jnp.concatenate([north[h, at(i), :] * f for h, f in enumerate(fs)], 1))
            for m, piece in enumerate((f_high, f_low, g_high, g_low)):
                pieces[at(i), m * cols:(m + 1) * cols] = piece

    def stage(s):
        held, fresh = (start, one, two)[s], (one, two, None)[s]

        def tile(n, c):
            t = lax.rem(n + last, tiles)

            @pl.when(n > 0 if s == 0 else n >= 0)
            def _():
                arrive(s, t)

            d = spread[at(t), :] * transport_step
            across[...] = jnp.dot(pieces[...], band[...], preferred_element_type=jnp.float32)
            split(held, lax.rem(t + 1, tiles))

            borders = []
            for side in range(2):
                halo = landed[s, t, side]
                total = None
                for k in range(1, REACH + 1):
                    inside = slot >= SLOT - k if side == 0 else slot < k
                    part = (jnp.where(inside, sixth_second[k - 1] * d, 0.0) + flows[side * REACH + k - 1]) * halo
                    if k < REACH:
                        part = pltpu.roll(part, (k - REACH) % LANES if side == 0 else REACH - k, 1)
                    total = part if total is None else total + part
                borders.append(total)
            ids = t * 8 + lax.broadcasted_iota(jnp.int32, (8, LANES), 0)
            reach = sixth_second[0] * d

            for b in range(rows // 8):
                for h in range(parts):
                    lanes = slice(h * LANES, (h + 1) * LANES)
                    f = [held[t * parts + h, at(b * 8 + m), :] for m in range(8 + 2 * REACH)]
                    gs = [east[h, at(b * 8 + m), :] * f[m] for m in range(8 + 2 * REACH)]
                    for r in range(8):
                        i = b * 8 + r
                        m = r + REACH
                        lap = (sixth_center / sixth_second[0]) * f[m] + (f[m + 1] + f[m - 1])
                        grad = gs[m + 1] - gs[m - 1]
                        for k in range(2, REACH + 1):
                            lap = lap + (sixth_second[k - 1] / sixth_second[0]) * (f[m + k] + f[m - k])
                            grad = grad + (sixth_first[k - 1] / sixth_first[0]) * (gs[m + k] - gs[m - k])
                        change = across[at(i), lanes] + (reach * lap - grad)
                        if h == 0:
                            change = change + jnp.where(
                                lane < REACH, pltpu.roll(borders[0], (LANES - home - SLOT * i - 1) % LANES, 1), 0.0)
                        if h == parts - 1:
                            change = change + jnp.where(
                                lane >= LANES - REACH,
                                pltpu.roll(borders[1], (2 * LANES - REACH - SLOT * i) % LANES, 1), 0.0)
                        if s == 0:
                            fresh[t * parts + h, at(REACH + i), :] = f[m] + change
                        elif s == 1:
                            fresh[t * parts + h, at(REACH + i), :] = (
                                0.75 * start[t * parts + h, at(REACH + i), :] + 0.25 * (f[m] + change))
                        else:
                            value = start[t * parts + h, at(REACH + i), :] * (1.0 / 3.0) + (2.0 / 3.0) * (f[m] + change)
                            out[t * parts + h, at(i), :] = jnp.where(ids < species, jnp.maximum(value, 0.0), value)
            if s < 2:
                pack(s + 1, t)
            return c

        split(held, last)
        lax.fori_loop(0, tiles, tile, 0)

    for s in range(3):
        stage(s)

    def finish(t, c):
        for s in range(3):
            for copy in copies(s, t):
                copy.wait_send()
        return c

    lax.fori_loop(0, tiles, finish, 0)


def band_matrix(width):
    here = np.arange(width)
    lag = here[:, None] - here[None, :]
    second = np.where(lag == 0, round(sixth_center * SECOND_SCALE), 0)
    first = np.zeros((width, width))
    for k in range(1, REACH + 1):
        ahead, behind = lag == k, lag == -k
        second = np.where(ahead | behind, round(sixth_second[k - 1] * SECOND_SCALE), second)
        weight = round(sixth_first[k - 1] * FIRST_SCALE)
        first = np.where(ahead, weight, np.where(behind, -weight, first))
    return jnp.asarray(np.concatenate([second, second, first, first], 0), jnp.bfloat16)


def advect(density, warm, leading, trailing, diffusion, pair, scaler, energy, produced, counts):
    species, rows, cols = density.shape
    fields = species + 1
    tiles = (fields + 2) // 8
    if (fields + 2) % 8 or rows * SLOT > LANES or cols % LANES or rows % 8:
        raise ValueError("unsupported sizes")
    parts = cols // LANES
    sizes = (lax.axis_size("grp"), lax.axis_size("gx"))
    vmem = pl.BlockSpec(memory_space=pltpu.VMEM)
    wide = pltpu.VMEM((tiles * parts, (rows + 2 * REACH) * 8, LANES), jnp.float32)
    band = band_matrix(cols)
    reactions = pair.shape[1]
    if counts.shape[1] > LANES or species > 64:
        raise ValueError("unsupported sizes")
    length = up(up(reactions, TRIPS), 8)
    weight = spread_weights(reactions)[None]
    smem = pl.BlockSpec(memory_space=pltpu.SMEM)
    return pl.pallas_call(
        functools.partial(advect_kernel, fields, sizes),
        in_specs=[vmem] * 4 + [smem] + [vmem] * 7,
        out_specs=[vmem] * 5,
        out_shape=[jax.ShapeDtypeStruct((tiles * parts, rows * 8, LANES), jnp.float32),
                   jax.ShapeDtypeStruct((3 * length, LANES), jnp.float32),
                   jax.ShapeDtypeStruct((2 * up(species, 8), up(length, 16)), jnp.bfloat16),
                   jax.ShapeDtypeStruct((1, 2 * up(length, LANES)), jnp.int32),
                   jax.ShapeDtypeStruct((1, LANES), jnp.int32)],
        scratch_shapes=[pltpu.VMEM((8, up(length, LANES)), jnp.float32),
                        pltpu.VMEM((tiles * 8, LANES), jnp.float32), wide, wide, wide,
                        pltpu.VMEM((parts, (rows + 2 * REACH) * 8, LANES), jnp.float32),
                        pltpu.VMEM((parts, rows * 8, LANES), jnp.float32),
                        pltpu.VMEM((rows * 8, 4 * cols), jnp.bfloat16),
                        pltpu.VMEM((rows * 8, cols), jnp.float32),
                        pltpu.VMEM((3, tiles, 2, 8, LANES), jnp.float32),
                        pltpu.VMEM((3, tiles, 2, 8, LANES), jnp.float32),
                        pltpu.VMEM((2 * REACH, 8, LANES), jnp.float32),
                        pltpu.SemaphoreType.DMA((3, tiles, 4)),
                        pltpu.SemaphoreType.DMA((3, tiles, 4))],
        compiler_params=pltpu.CompilerParams(collective_id=0, has_side_effects=True, vmem_limit_bytes=ROOM),
        name="advect",
    )(density.reshape(species * rows, cols), warm, leading, trailing, diffusion, band, pair, scaler, energy, produced,
      weight, counts)


GROUP = 16
PITCH = GROUP + 1
SPAN = 9


def chemistry_kernel(species, chunk, order, counts, pair, warming, rates, table, state, out, warm_out,
                     held, low_gained, high_gained, progress, steps, staged, sems, *losses):
    rows, cols = warm_out.shape
    layers = state.shape[0] * LANES // cols * 8
    per_row = cols // TILE
    tiles = rows * per_row
    warm_row = species
    length = rates.shape[0] // 3
    reactions = length // chunk * chunk
    span = progress.shape[0] // GROUP
    depth = table.shape[1]
    half = table.shape[0] // 2
    blocks = layers // 8
    lines = staged.reshape(staged.shape[0] * staged.shape[1], LANES)
    line_span = staged.shape[1]
    gained = (low_gained, high_gained)

    for t in range(GROUP):
        progress[pl.ds(t * span + reactions, depth - reactions)] = jnp.zeros((depth - reactions, LANES), jnp.float32)
    for loss in losses:
        loss[...] = jnp.zeros_like(loss)

    def at(field):
        return pl.ds(field * PITCH, GROUP)

    def handle(g, c):
        ids = [order[0, g * GROUP + t] for t in range(GROUP)]
        numbers = [counts[t] for t in ids]
        places = [(t % per_row, pl.ds(pl.multiple_of(t // per_row * 8, 8), 8)) for t in ids]
        turn_count = functools.reduce(jnp.maximum, numbers)
        for t in range(GROUP):
            part, at_row = places[t]
            steps[t:t + 1, :] = jnp.full((1, LANES), numbers[t].astype(jnp.float32))
            for f in range(blocks):
                held[pl.ds(f * 8 * PITCH + t, 8, stride=PITCH)] = state[f * per_row + part, at_row, :]

        def advance(s, c):
            heat = jnp.tanh(held[at(warm_row)])

            def react(k, c):
                for j in range(chunk):
                    r = k * chunk + j
                    first = pl.ds(pair[0, r], GROUP)
                    second = pl.ds(pair[0, pair.shape[1] // 2 + r], GROUP)
                    a, e, weight = [jnp.broadcast_to(rates[pl.ds(n * length + r, 1), :], (GROUP, LANES)) for n in range(3)]
                    rate = jnp.exp2(a + e * heat)
                    ca, cb = held[first], held[second]
                    qa, qb = rate * ca, rate * cb
                    progress[pl.ds(r, GROUP, stride=span)] = qa * (weight * cb)
                    n = 2 * (j % (len(losses) // 2))
                    losses[n][first] += qb
                    losses[n + 1][second] += qa
                return c

            lax.fori_loop(0, reactions // chunk, react, 0)
            for n, fill in enumerate(gained):
                for q in range(4 * n, 4 * n + 4):
                    p = jnp.concatenate([progress[pl.ds((2 * q + t) * span, depth)] for t in range(2)], 1)
                    both = jnp.dot(table[...], p.astype(jnp.bfloat16), preferred_element_type=jnp.float32)
                    total = both[:half] + both[half:]
                    for t in range(2):
                        for f in range(half // 8):
                            fill[pl.ds(f * 8 * SPAN + 2 * (q - 4 * n) + t, 8, stride=SPAN)] = (
                                total[f * 8:(f + 1) * 8, t * TILE:(t + 1) * TILE])
                number = steps[8 * n:8 * n + 8, :]
                pace = number * (1.0 / chemistry_span)
                active = s.astype(jnp.float32) < number
                change = jnp.zeros((8, LANES), jnp.float32)
                for j in range(species):
                    place = pl.ds(j * PITCH + 8 * n, 8)
                    x = held[place]
                    destroyed = functools.reduce(jnp.add, [loss[place] for loss in losses])
                    for loss in losses:
                        loss[place] = jnp.zeros((8, LANES), jnp.float32)
                    updated = (pace * x + fill[pl.ds(j * SPAN, 8)]) / (pace + destroyed)
                    change = change + warming[j] * (updated - x)
                    held[place] = jnp.where(active, updated, x)
                place = pl.ds(warm_row * PITCH + 8 * n, 8)
                w = held[place]
                held[place] = jnp.where(active, w + change, w)
            return c

        lax.fori_loop(0, turn_count, advance, 0)
        for t in range(GROUP):
            line = (ids[t] % per_row) * ((warm_row + 1) * line_span) + ids[t] // per_row
            for f in range(0, warm_row + 1, 8):
                n = min(8, warm_row + 1 - f)
                lines[pl.ds(line + f * line_span, n, stride=line_span)] = held[pl.ds(f * PITCH + t, n, stride=PITCH)]
        return c

    lax.fori_loop(0, tiles // GROUP, handle, 0)
    wide = out.reshape(species, rows, cols)
    copies = []
    for n in range(per_row):
        lanes = pl.ds(n * TILE, TILE)
        first = n * (warm_row + 1)
        copies.append(pltpu.make_async_copy(
            staged.at[pl.ds(first, species), pl.ds(0, rows)], wide.at[:, :, lanes], sems.at[0, n]))
        copies.append(pltpu.make_async_copy(
            staged.at[first + species, pl.ds(0, rows)], warm_out.at[:, lanes], sems.at[1, n]))
    for copy in copies:
        copy.start()
    for copy in copies:
        copy.wait()


LOSSES = 4


def chemistry(state, order, counts, pair, warming, rates, table, species, rows, cols):
    layers = state.shape[0] * LANES // cols * 8
    smem = pl.BlockSpec(memory_space=pltpu.SMEM)
    vmem = pl.BlockSpec(memory_space=pltpu.VMEM)
    block = pltpu.VMEM((layers * PITCH, LANES), jnp.float32)
    part = pltpu.VMEM((layers * SPAN, LANES), jnp.float32)
    return pl.pallas_call(
        functools.partial(chemistry_kernel, species, rates.shape[0] // 3 // TRIPS),
        in_specs=[smem, smem, smem, smem, vmem, vmem, vmem],
        out_specs=[pl.BlockSpec(memory_space=pl.ANY)] * 2,
        out_shape=[jax.ShapeDtypeStruct((species * rows, cols), jnp.float32),
                   jax.ShapeDtypeStruct((rows, cols), jnp.float32)],
        scratch_shapes=[block, part, part,
                        pltpu.VMEM((GROUP * (table.shape[1] + 1), LANES), jnp.float32),
                        pltpu.VMEM((GROUP, LANES), jnp.float32),
                        pltpu.VMEM((cols // TILE * (species + 1), rows + 8, TILE), jnp.float32),
                        pltpu.SemaphoreType.DMA((2, cols // TILE))]
        + [block] * LOSSES,
        compiler_params=pltpu.CompilerParams(vmem_limit_bytes=ROOM),
        name="chemistry",
    )(order, counts, pair, warming, rates, table, state)


def body(component_density, scaled_thermal_state, leading_direction_flow, trailing_direction_flow,
         spreading_coefficient, colliding_pair, natural_exponent_scaler, arrhenius_energy,
         stoichiometric_output, formation_warming, explicit_increments):
    species, rows, cols = component_density.shape
    clipped, rates, table, pair, order = advect(
        component_density, scaled_thermal_state, leading_direction_flow, trailing_direction_flow, spreading_coefficient,
        colliding_pair.T, natural_exponent_scaler, arrhenius_energy, stoichiometric_output.T,
        explicit_increments[None])
    reacted, warm = chemistry(clipped, order, explicit_increments, pair, formation_warming, rates, table,
                              species, rows, cols)
    return reacted.reshape(species, rows, cols), warm


def solution(mesh):
    return jax.shard_map(
        body,
        mesh=mesh,
        in_specs=(
            P(None, "gx", "grp"),
            P("gx", "grp"),
            P("gx", "grp"),
            P("gx", "grp"),
            P(),
            P(),
            P(),
            P(),
            P(),
            P(),
            P(("grp", "gx")),
        ),
        out_specs=(P(None, "gx", "grp"), P("gx", "grp")),
        check_vma=False,
    )
```

profile of v0, /device:TPU:20, one launch (start us, length us, event | category | flops | bytes accessed | tf_op | source)
XLA Modules:
  0.0 60.6 jit_solution(6081762755423018743)
XLA Ops:
  0.6 0.0 copy-start.12
  0.6 0.0 copy-start
  0.7 1.5 %copy-done = f32[53,32,256]{2,1,0:T(8,128)S(1)} copy-done((f32[53,32,256]{2,1,0:T(8,128)S(1)}, f32[53,32,256]{2,1,0:T(8,128)}, u32[]{:S(2)}) %copy-start) | copy-done | bytes 1736728
  2.1 0.0 copy-start.1
  2.1 1.0 %copy-done.1 = bf16[1024,256]{1,0:T(8,128)(2,1)S(1)} copy-done((bf16[1024,256]{1,0:T(8,128)(2,1)S(1)}, bf16[1024,256]{1,0:T(8,128)(2,1)}, u32[]{:S(2)}) %copy-start.1) | copy-done | bytes 524312
  3.2 0.0 copy-start.2
  3.2 0.9 %copy-done.2 = f32[325,53]{0,1:T(8,128)S(1)} copy-done((f32[325,53]{0,1:T(8,128)S(1)}, f32[325,53]{0,1:T(8,128)}, u32[]{:S(2)}) %copy-start.2) | copy-done | bytes 68924
  4.0 0.0 copy-start.3
  4.0 0.8 %copy-done.3 = f32[32,256]{1,0:T(8,128)S(1)} copy-done((f32[32,256]{1,0:T(8,128)S(1)}, f32[32,256]{1,0:T(8,128)}, u32[]{:S(2)}) %copy-start.3) | copy-done | bytes 32792
  4.8 0.0 copy-start.4
  4.8 0.8 %copy-done.4 = f32[32,256]{1,0:T(8,128)S(1)} copy-done((f32[32,256]{1,0:T(8,128)S(1)}, f32[32,256]{1,0:T(8,128)}, u32[]{:S(2)}) %copy-start.4) | copy-done | bytes 32792
  5.6 0.0 copy-start.5
  5.6 0.8 %copy-done.5 = f32[32,256]{1,0:T(8,128)S(1)} copy-done((f32[32,256]{1,0:T(8,128)S(1)}, f32[32,256]{1,0:T(8,128)}, u32[]{:S(2)}) %copy-start.5) | copy-done | bytes 32792
  6.3 0.0 copy-start.6
  6.3 0.7 %copy-done.6 = s32[325,2]{0,1:T(2,128)S(1)} copy-done((s32[325,2]{0,1:T(2,128)S(1)}, s32[325,2]{0,1:T(2,128)}, u32[]{:S(2)}) %copy-start.6) | copy-done | bytes 2624
  7.0 0.0 copy-start.7
  7.0 0.7 %copy-done.7 = f32[325]{0:T(512)S(1)} copy-done((f32[325]{0:T(512)S(1)}, f32[325]{0:T(512)}, u32[]{:S(2)}) %copy-start.7) | copy-done | bytes 1324
  7.7 0.7 %copy-done.8 = f32[325]{0:T(512)S(1)} copy-done((f32[325]{0:T(512)S(1)}, f32[325]{0:T(512)}, u32[]{:S(2)}) %copy-start.8) | copy-done | bytes 1324
  8.4 0.7 %copy-done.9 = s32[64]{0:T(128)S(1)} copy-done((s32[64]{0:T(128)S(1)}, s32[64]{0:T(128)}, u32[]{:S(2)}) %copy-start.9) | copy-done | bytes 280
  9.0 0.7 %copy-done.10 = f32[1,325]{1,0:T(1,128)S(1)} copy-done((f32[1,325]{1,0:T(1,128)S(1)}, f32[1,325]{1,0:T(1,128)}, u32[]{:S(2)}) %copy-start.10) | copy-done | bytes 1324
  9.7 0.7 %copy-done.11 = f32[54]{0:T(128)S(1)} copy-done((f32[54]{0:T(128)S(1)}, f32[54]{0:T(128)}, u32[]{:S(2)}) %copy-start.11) | copy-done | bytes 240
  10.4 21.9 %advect.1 = (f32[14,256,128]{2,1,0:T(8,128)S(1)}, f32[984,128]{1,0:T(8,128)S(1)}, bf16[112,336]{1,0:T(8,128)(2,1)S(1)}, s32[1,768]{1,0:T(1,128)S(1)}, s32[1,128]{1,0:T(1,128)S(1)}) custom-call(f32[1696,256]{1,0:T(8,128)S(1)} %bitcast.5, f32[32,256]{1,0:T(8,128)S(1)} %copy-done.3, f32[32,256]{1,0:T(8,128)S(1)} %copy-done.4, f32[32,256]{1,0:T(8,128)S(1)} %copy-done.5, ...), custom_call_target="tpu_custom_call" | custom-call | tf_op jit(solution)/shard_map/advect/pallas_call | solution.py:305
  32.2 0.0 copy-done.12
  32.3 28.3 %chemistry.1 = (f32[1696,256]{1,0:T(8,128)}, f32[32,256]{1,0:T(8,128)}) custom-call(s32[1,128]{1,0:T(1,128)S(1)} %get-tuple-element.9.order, s32[64]{0:T(128)S(1)} %copy-done.9, s32[1,768]{1,0:T(1,128)S(1)} %get-tuple-element.10.pair, f32[53]{0:T(128)S(1)} %copy-done.12, f32[984,128]{1,0:T(8,128)S(1)} %get-tuple-element.11.rates, ...), custom_call_target="tpu_custom_call" | custom-call | tf_op jit(solution)/shard_map/chemistry/pallas_call | solution.py:451
  (4 shorter events, 0.0 us)
Async XLA Ops:
  0.6 31.6 %copy-start.12 = (f32[53]{0:T(128)S(1)}, f32[53]{0:T(128)}, u32[]{:S(2)}) copy-start(f32[53]{0:T(128)} %warming.1) | copy-start | bytes 640
  0.6 1.5 %copy-start = (f32[53,32,256]{2,1,0:T(8,128)S(1)}, f32[53,32,256]{2,1,0:T(8,128)}, u32[]{:S(2)}) copy-start(f32[53,32,256]{2,1,0:T(8,128)} %param.13) | copy-start | bytes 5210116
  2.1 1.0 %copy-start.1 = (bf16[1024,256]{1,0:T(8,128)(2,1)S(1)}, bf16[1024,256]{1,0:T(8,128)(2,1)}, u32[]{:S(2)}) copy-start(bf16[1024,256]{1,0:T(8,128)(2,1)} %constant.4.clone.band) | copy-start | bytes 1572868
  3.2 0.9 %copy-start.2 = (f32[325,53]{0,1:T(8,128)S(1)}, f32[325,53]{0,1:T(8,128)}, u32[]{:S(2)}) copy-start(f32[325,53]{0,1:T(8,128)} %param.21) | copy-start | bytes 206704
  4.0 0.8 %copy-start.3 = (f32[32,256]{1,0:T(8,128)S(1)}, f32[32,256]{1,0:T(8,128)}, u32[]{:S(2)}) copy-start(f32[32,256]{1,0:T(8,128)} %warm.1) | copy-start | bytes 98308
  4.8 0.8 %copy-start.4 = (f32[32,256]{1,0:T(8,128)S(1)}, f32[32,256]{1,0:T(8,128)}, u32[]{:S(2)}) copy-start(f32[32,256]{1,0:T(8,128)} %leading.1) | copy-start | bytes 98308
  5.6 0.8 %copy-start.5 = (f32[32,256]{1,0:T(8,128)S(1)}, f32[32,256]{1,0:T(8,128)}, u32[]{:S(2)}) copy-start(f32[32,256]{1,0:T(8,128)} %trailing.1) | copy-start | bytes 98308
  6.3 0.7 %copy-start.6 = (s32[325,2]{0,1:T(2,128)S(1)}, s32[325,2]{0,1:T(2,128)}, u32[]{:S(2)}) copy-start(s32[325,2]{0,1:T(2,128)} %param.18) | copy-start | bytes 7804
  7.0 0.7 %copy-start.7 = (f32[325]{0:T(512)S(1)}, f32[325]{0:T(512)}, u32[]{:S(2)}) copy-start(f32[325]{0:T(512)} %scaler.1) | copy-start | bytes 3904
  7.7 0.7 %copy-start.8 = (f32[325]{0:T(512)S(1)}, f32[325]{0:T(512)}, u32[]{:S(2)}) copy-start(f32[325]{0:T(512)} %energy.1) | copy-start | bytes 3904
  8.4 0.7 %copy-start.9 = (s32[64]{0:T(128)S(1)}, s32[64]{0:T(128)}, u32[]{:S(2)}) copy-start(s32[64]{0:T(128)} %counts.1) | copy-start | bytes 772
  9.0 0.7 %copy-start.10 = (f32[1,325]{1,0:T(1,128)S(1)}, f32[1,325]{1,0:T(1,128)}, u32[]{:S(2)}) copy-start(f32[1,325]{1,0:T(1,128)} %constant.5.clone.weight) | copy-start | bytes 3904
  9.7 0.7 %copy-start.11 = (f32[54]{0:T(128)S(1)}, f32[54]{0:T(128)}, u32[]{:S(2)}) copy-start(f32[54]{0:T(128)} %diffusion.1) | copy-start | bytes 652
where the time goes:
time: 61.5 us; the launch traced here: 60.6 us
  Pallas kernels  50.2 us (82%)
  local copies, waits for them, and re-layouts  9.7 us (16%)
  between operations  0.68 us (1%)
    pallas_call x1, Pallas kernels, chemistry(): pl.pallas_call(functools.partial(chemistry_kernel, species, rates.shape[0...  28.3 us
    pallas_call x1, Pallas kernels, advect(): pl.pallas_call(functools.partial(advect_kernel, fields, sizes), in_specs=...  21.9 us
    unnamed x26, local copies, waits for them, and re-layouts  9.7 us

commit v1 on v0

--- a/solution.py
+++ b/solution.py
@@ -33,7 +33,6 @@
 LANES = 128
 NEVER = -16384.0
 TRIPS = 3
-ROOM = 32 << 20
 
 
 def halves(value):
@@ -77,9 +76,13 @@
     order[...] = jnp.sum(here, axis=0, keepdims=True).astype(jnp.int32)
 
 
-def advect_kernel(fields, sizes, density, warm, leading, trailing, diffusion, band, pair, scaler, energy, produced,
-                  weight, counts, out, rates, table, offsets, order,
-                  lines, spread, start, one, two, east, north, pieces, across, packed, landed, flows, send, recv):
+def advect_kernel(fields, sizes, sources, targets, scratch):
+    (out, rates, table, offsets, order, stored, density, warm, leading, trailing, diffusion, band, pair, scaler, energy, produced, weight, counts, loaded,
+     lines, spread, start, one, two, east, north, pieces, across, packed, landed, flows, send, recv) = scratch
+    inputs = [pltpu.make_async_copy(src, dst, loaded.at[n]) for n, (src, dst) in enumerate(
+        zip(sources, (density, warm, leading, trailing, diffusion, band, pair, scaler, energy, produced, weight, counts)))]
+    for copy in inputs:
+        copy.start()
     n_grp, n_gx = sizes
     g, x = lax.axis_index("grp"), lax.axis_index("gx")
     rows, cols = warm.shape
@@ -111,6 +114,10 @@
     def of_plane(ref):
         return lambda q, h: ref[q * 8:(q + 1) * 8, h * LANES:(h + 1) * LANES]
 
+    def result(t):
+        both = pl.ds(t * parts, parts)
+        return pltpu.make_async_copy(out.at[both], targets[0].at[both], stored.at[t])
+
     def copies(s, t):
         held = (start, one, two)[s]
         both = pl.ds(t * parts, parts)
@@ -145,6 +152,8 @@
         for copy in copies(s, t):
             copy.start()
 
+    for copy in inputs:
+        copy.wait()
     for f in range(tiles * 8):
         spread[f:f + 1, :] = jnp.full((1, LANES), diffusion[f] if f < fields else 0.0)
     for f in range(last * 8, species):
@@ -174,6 +183,10 @@
             copy.wait_recv()
 
     prepare_tables(pair, scaler, energy, produced, weight, counts, rates, table, offsets, order, lines)
+    tables = [pltpu.make_async_copy(src, dst, stored.at[tiles + n]) for n, (src, dst) in enumerate(
+        zip((rates, table, offsets, order), targets[1:]))]
+    for copy in tables:
+        copy.start()
     arrive(0, last)
     u_sub, v_sub = fields % 8, (fields + 1) % 8
     for r in (*range(REACH), *range(REACH + rows, 2 * REACH + rows)):
@@ -255,6 +268,8 @@
                             out[t * parts + h, at(i), :] = jnp.where(ids < species, jnp.maximum(value, 0.0), value)
             if s < 2:
                 pack(s + 1, t)
+            else:
+                result(t).start()
             return c
 
         split(held, last)
@@ -263,7 +278,11 @@
     for s in range(3):
         stage(s)
 
+    for copy in tables:
+        copy.wait()
+
     def finish(t, c):
+        result(t).wait()
         for s in range(3):
             for copy in copies(s, t):
                 copy.wait_send()
@@ -293,7 +312,6 @@
         raise ValueError("unsupported sizes")
     parts = cols // LANES
     sizes = (lax.axis_size("grp"), lax.axis_size("gx"))
-    vmem = pl.BlockSpec(memory_space=pltpu.VMEM)
     wide = pltpu.VMEM((tiles * parts, (rows + 2 * REACH) * 8, LANES), jnp.float32)
     band = band_matrix(cols)
     reactions = pair.shape[1]
@@ -301,31 +319,43 @@
         raise ValueError("unsupported sizes")
     length = up(up(reactions, TRIPS), 8)
     weight = spread_weights(reactions)[None]
-    smem = pl.BlockSpec(memory_space=pltpu.SMEM)
+    args = (density.reshape(species * rows, cols), warm, leading, trailing, diffusion, band, pair, scaler, energy, produced,
+            weight, counts)
+    count = len(args)
+    places = [pltpu.SMEM if n == 4 else pltpu.VMEM for n in range(count)]
+
+    results = [jax.ShapeDtypeStruct((tiles * parts, rows * 8, LANES), jnp.float32),
+               jax.ShapeDtypeStruct((3 * length, LANES), jnp.float32),
+               jax.ShapeDtypeStruct((2 * up(species, 8), up(length, 16)), jnp.bfloat16),
+               jax.ShapeDtypeStruct((1, 2 * up(length, LANES)), jnp.int32),
+               jax.ShapeDtypeStruct((1, LANES), jnp.int32)]
+
+    def kernel(*refs):
+        advect_kernel(fields, sizes, refs[:count], refs[count:count + len(results)], refs[count + len(results):])
+
     return pl.pallas_call(
-        functools.partial(advect_kernel, fields, sizes),
-        in_specs=[vmem] * 4 + [smem] + [vmem] * 7,
-        out_specs=[vmem] * 5,
-        out_shape=[jax.ShapeDtypeStruct((tiles * parts, rows * 8, LANES), jnp.float32),
-                   jax.ShapeDtypeStruct((3 * length, LANES), jnp.float32),
-                   jax.ShapeDtypeStruct((2 * up(species, 8), up(length, 16)), jnp.bfloat16),
-                   jax.ShapeDtypeStruct((1, 2 * up(length, LANES)), jnp.int32),
-                   jax.ShapeDtypeStruct((1, LANES), jnp.int32)],
-        scratch_shapes=[pltpu.VMEM((8, up(length, LANES)), jnp.float32),
-                        pltpu.VMEM((tiles * 8, LANES), jnp.float32), wide, wide, wide,
-                        pltpu.VMEM((parts, (rows + 2 * REACH) * 8, LANES), jnp.float32),
-                        pltpu.VMEM((parts, rows * 8, LANES), jnp.float32),
-                        pltpu.VMEM((rows * 8, 4 * cols), jnp.bfloat16),
-                        pltpu.VMEM((rows * 8, cols), jnp.float32),
-                        pltpu.VMEM((3, tiles, 2, 8, LANES), jnp.float32),
-                        pltpu.VMEM((3, tiles, 2, 8, LANES), jnp.float32),
-                        pltpu.VMEM((2 * REACH, 8, LANES), jnp.float32),
-                        pltpu.SemaphoreType.DMA((3, tiles, 4)),
-                        pltpu.SemaphoreType.DMA((3, tiles, 4))],
-        compiler_params=pltpu.CompilerParams(collective_id=0, has_side_effects=True, vmem_limit_bytes=ROOM),
+        kernel,
+        in_specs=[pl.BlockSpec(memory_space=pltpu.HBM)] * count,
+        out_specs=[pl.BlockSpec(memory_space=pltpu.HBM)] * len(results),
+        out_shape=results,
+        scratch_shapes=[pltpu.VMEM(result.shape, result.dtype) for result in results]
+        + [pltpu.SemaphoreType.DMA((tiles + len(results) - 1,))]
+        + [place(arg.shape, arg.dtype) for place, arg in zip(places, args)]
+        + [pltpu.SemaphoreType.DMA((count,)),
+           pltpu.VMEM((8, up(length, LANES)), jnp.float32),
+           pltpu.VMEM((tiles * 8, LANES), jnp.float32), wide, wide, wide,
+           pltpu.VMEM((parts, (rows + 2 * REACH) * 8, LANES), jnp.float32),
+           pltpu.VMEM((parts, rows * 8, LANES), jnp.float32),
+           pltpu.VMEM((rows * 8, 4 * cols), jnp.bfloat16),
+           pltpu.VMEM((rows * 8, cols), jnp.float32),
+           pltpu.VMEM((3, tiles, 2, 8, LANES), jnp.float32),
+           pltpu.VMEM((3, tiles, 2, 8, LANES), jnp.float32),
+           pltpu.VMEM((2 * REACH, 8, LANES), jnp.float32),
+           pltpu.SemaphoreType.DMA((3, tiles, 4)),
+           pltpu.SemaphoreType.DMA((3, tiles, 4))],
+        compiler_params=pltpu.CompilerParams(collective_id=0, has_side_effects=True),
         name="advect",
-    )(density.reshape(species * rows, cols), warm, leading, trailing, diffusion, band, pair, scaler, energy, produced,
-      weight, counts)
+    )(*args)
 
 
 GROUP = 16
@@ -460,7 +490,6 @@
                         pltpu.VMEM((cols // TILE * (species + 1), rows + 8, TILE), jnp.float32),
                         pltpu.SemaphoreType.DMA((2, cols // TILE))]
         + [block] * LOSSES,
-        compiler_params=pltpu.CompilerParams(vmem_limit_bytes=ROOM),
         name="chemistry",
     )(order, counts, pair, warming, rates, table, state)
 

time: 61.5 us -> 53.5 us (0.87)
  the two profiles are of different devices: /device:TPU:20 before, /device:TPU:0 now
where the time goes in v1:
time: 53.5 us; the launch traced here: 54 us
  Pallas kernels  53.4 us (100%)
  between operations  0.64 us (1%)
    pallas_call x1, Pallas kernels, chemistry(): pl.pallas_call(functools.partial(chemistry_kernel, species, rates.shape[0...  27.9 us
    pallas_call x1, Pallas kernels, advect(): pl.pallas_call(kernel, in_specs=[pl.BlockSpec(memory_space=pltpu.HBM)] *...  25.5 us

profile of v1, /device:TPU:0, one launch (start us, length us, event | category | flops | bytes accessed | tf_op | source)
XLA Modules:
  0.0 54.0 jit_solution(6435416454608606751)
XLA Ops:
  0.6 25.5 %advect.1 = (f32[14,256,128]{2,1,0:T(8,128)}, f32[984,128]{1,0:T(8,128)}, bf16[112,336]{1,0:T(8,128)(2,1)}, s32[1,768]{1,0:T(1,128)}, s32[1,128]{1,0:T(1,128)}) custom-call(f32[1696,256]{1,0:T(8,128)} %bitcast.5, f32[32,256]{1,0:T(8,128)} %refs_1_.1, f32[32,256]{1,0:T(8,128)} %refs_2_.1, f32[32,256]{1,0:T(8,128)} %refs_3_.1, f32[54]{0:T(128)} %refs_4_.1, ...), custom_call_target="tpu_custom_call" | custom-call | tf_op jit(solution)/shard_map/advect/pallas_call | solution.py:336
  26.1 27.9 %chemistry.1 = (f32[1696,256]{1,0:T(8,128)}, f32[32,256]{1,0:T(8,128)}) custom-call(s32[1,128]{1,0:T(1,128)} %get-tuple-element.9.order, s32[64]{0:T(128)} %counts.1, s32[1,768]{1,0:T(1,128)} %get-tuple-element.10.pair, f32[53]{0:T(128)} %warming.1, f32[984,128]{1,0:T(8,128)} %get-tuple-element.11.rates, bf16[112,336]{1,0:T(8,128)(2,1)} %get-tuple-element.12.table, ...), custom_call_target="tpu_custom_call" | custom-call | tf_op jit(solution)/shard_map/chemistry/pallas_call | solution.py:481
